TPU v7x, 32 devices: a whole 2x2x4 slice. The times are simulated.
32 devices in a mesh: dp: 4 (over z), neg: 8 (over y, x, core).
Axes of the slice: x: 2, y: 2, z: 4, core: 2. Of those that a mesh axis runs over, the one named last changes fastest.
Arguments:
- query_emb: bfloat16 [128, 32, 128], P(('dp', 'neg')), may hold values from -6 to 6
- positive: int32 [128], P(('dp', 'neg')), may hold values from 0 to 31
- passage_emb: bfloat16 [32, 512, 128], P(('dp', 'neg')), may hold values from -6 to 6
- lengths: int32 [32], P(('dp', 'neg')), may hold values from 256 to 512
- residual: bfloat16 [16384, 1024], P(('dp', 'neg')), may hold values from -6 to 6
- context: bfloat16 [16384, 1024], P(('dp', 'neg')), may hold values from -6 to 6
- out_proj: bfloat16 [1024, 1024], replicated, may hold values from -0.1875 to 0.1875
- norm_gain: float32 [1024], replicated, may hold values from 0.5 to 1.5
- colbert_proj: bfloat16 [1024, 128], replicated, may hold values from -0.1875 to 0.1875
Outputs:
- loss: float32 [], replicated
- query_grad: float32 [128, 32, 128], P(('dp', 'neg'))
- residual_grad: bfloat16 [16384, 1024], P(('dp', 'neg'))
- context_grad: bfloat16 [16384, 1024], P(('dp', 'neg'))
- out_proj_grad: float32 [1024, 1024], replicated
- colbert_grad: float32 [1024, 128], replicated
- gain_grad: float32 [1024], replicated
Inputs may be any that keep to these rules, and one draw needn't show every extreme that they name: A passage's first lengths[p] token slots are real, the rest padding.
All inputs are finite; a program needn't handle non-finite values.
Results may differ from a plain program's by a relative error of at most 0.0065.
Values may be sent and summed in bfloat16 or wider, within the bound.
A program may use at most 64 MiB of HBM per device.

v0:
```python
import math
import jax
import jax.numpy as jnp
from jax import lax
from jax.sharding import PartitionSpec as P


def combined_all(array, axis, combine):
    everything = jax.tree.map(lambda part: lax.all_gather(part, axis), array)
    initial = jax.tree.map(lambda part: part[0], everything)

    def turn(k, so_far):
        return combine(so_far, jax.tree.map(lambda part: part[k], everything))

    return lax.fori_loop(1, lax.axis_size(axis), turn, initial)


def block_plan(query_count, query_len):
    return math.gcd(query_count, max(1, 2048 // query_len))


def masked_scores(query_block, passage_one, usable):
    scores = jnp.einsum("rd,jd->rj", query_block, passage_one, preferred_element_type=jnp.float32)
    return jnp.where(usable, scores, -1e30)


def tile_forward(query_tokens, query_pos, passage_tokens, passage_len, passage_ids):
    query_count, query_len, emb_width = query_tokens.shape
    per_block = block_plan(query_count, query_len)
    query_blocks = query_tokens.reshape(query_count // per_block, per_block * query_len, emb_width)

    def per_passage(inputs):
        passage_one, length = inputs
        usable = (jnp.arange(passage_one.shape[0]) < length)[None, :]

        def per_query(query_block):
            masked = masked_scores(query_block, passage_one, usable)
            highest = jnp.max(masked, axis=1, keepdims=True)
            return highest[:, 0] + jnp.log(jnp.sum(jnp.exp(masked - highest), axis=1))

        inner_lse = lax.map(per_query, query_blocks).reshape(query_count, query_len)
        shifted = inner_lse - jnp.log(length.astype(jnp.float32))
        return (inner_lse, jnp.sum(shifted, axis=1))

    inner_all, similar = lax.map(per_passage, (passage_tokens, passage_len))
    similar = similar.T
    is_positive = passage_ids[None, :] == query_pos[:, None]
    highest = jnp.max(similar, axis=1)
    exp_total = jnp.sum(jnp.exp(similar - highest[:, None]), axis=1)
    positive_score = jnp.sum(jnp.where(is_positive, similar, 0.0), axis=1)
    return (inner_all, similar, is_positive, (highest, exp_total, positive_score))


def combine_totals(earlier, later):
    highest = jnp.maximum(earlier[0], later[0])
    exp_total = earlier[1] * jnp.exp(earlier[0] - highest) + later[1] * jnp.exp(later[0] - highest)
    return (highest, exp_total, earlier[2] + later[2])


def finish_rows(similar, is_positive, totals, own_block, query_dev):
    log_total = totals[0] + jnp.log(totals[1])
    coefficient = jnp.exp(similar - log_total[:, None]) - is_positive.astype(jnp.float32)
    own_terms = lax.dynamic_slice_in_dim(log_total - totals[2], own_block * query_dev, query_dev)
    return (coefficient, jnp.sum(own_terms))


def tile_backward(query_tokens, passage_tokens, passage_len, inner_all, coefficient):
    query_count, query_len, emb_width = query_tokens.shape
    per_block = block_plan(query_count, query_len)
    block_count = query_count // per_block
    query_blocks = query_tokens.reshape(block_count, per_block * query_len, emb_width)

    def per_passage(running, inputs):
        passage_one, length, inner_lse, column = inputs
        usable = (jnp.arange(passage_one.shape[0]) < length)[None, :]

        def per_query(pieces):
            query_block, inner_block, column_block = pieces
            masked = masked_scores(query_block, passage_one, usable)
            spread = jnp.exp(masked - inner_block.reshape(-1)[:, None]).reshape(
                per_block, query_len, -1
            )
            weight = (
                (spread * column_block[:, None, None])
                .reshape(per_block * query_len, -1)
                .astype(jnp.bfloat16)
            )
            query_part = jnp.dot(weight, passage_one, preferred_element_type=jnp.float32)
            passage_part = jnp.einsum(
                "rj,rd->jd", weight, query_block, preferred_element_type=jnp.float32
            )
            return (query_part, passage_part)

        query_parts, passage_parts = lax.map(
            per_query,
            (
                query_blocks,
                inner_lse.reshape(block_count, per_block, query_len),
                column.reshape(block_count, per_block),
            ),
        )
        return (running + query_parts.reshape(running.shape), jnp.sum(passage_parts, axis=0))

    start = jnp.zeros((query_count * query_len, emb_width), jnp.float32)
    query_sum, passage_sum = lax.scan(
        per_passage, start, (passage_tokens, passage_len, inner_all, coefficient.T)
    )
    return (query_sum.reshape(query_count, query_len, emb_width), passage_sum)


def window_rows(resid_rows, context_rows, grad_rows, out_proj, norm_gain, colbert_proj):
    hidden = resid_rows.astype(jnp.float32) + jnp.dot(
        context_rows, out_proj, preferred_element_type=jnp.float32
    )
    row_mean = jnp.mean(hidden, axis=1, keepdims=True)
    centred = hidden - row_mean
    variance = jnp.mean(centred * centred, axis=1, keepdims=True)
    inv_std = 1.0 / jnp.sqrt(variance + 1e-05)
    normed = centred * inv_std
    scaled = (normed * norm_gain).astype(jnp.bfloat16)
    colbert_part = jnp.dot(scaled.T, grad_rows, preferred_element_type=jnp.float32)
    scaled_grad = jnp.dot(grad_rows, colbert_proj.T, preferred_element_type=jnp.float32)
    gain_part = jnp.sum(scaled_grad * normed, axis=0)
    gained = scaled_grad * norm_gain
    hidden_grad = (
        inv_std
        * (
            gained
            - jnp.mean(gained, axis=1, keepdims=True)
            - normed * jnp.mean(gained * normed, axis=1, keepdims=True)
        )
    ).astype(jnp.bfloat16)
    context_grad = jnp.dot(hidden_grad, out_proj.T, preferred_element_type=jnp.float32).astype(
        jnp.bfloat16
    )
    proj_part = jnp.dot(context_rows.T, hidden_grad, preferred_element_type=jnp.float32)
    return (hidden_grad, context_grad, proj_part, colbert_part, gain_part)


def body(
    query_emb, positive, passage_emb, lengths, residual, context, out_proj, norm_gain, colbert_proj
):
    query_dev = query_emb.shape[0]
    passage_dev = passage_emb.shape[0]
    neg_size = lax.axis_size("neg")
    neg_place = lax.axis_index("neg")
    query_tokens, query_pos = (
        lax.all_gather(query_emb, "neg", axis=0, tiled=True),
        lax.all_gather(positive, "neg", axis=0, tiled=True),
    )
    passage_tokens, passage_len = (
        lax.all_gather(passage_emb, "dp", axis=0, tiled=True),
        lax.all_gather(lengths, "dp", axis=0, tiled=True),
    )
    position = jnp.arange(passage_tokens.shape[0], dtype=jnp.int32)
    passage_ids = (
        position // passage_dev * neg_size + neg_place
    ) * passage_dev + position % passage_dev
    inner_all, similar, is_positive, stats = tile_forward(
        query_tokens, query_pos, passage_tokens, passage_len, passage_ids
    )
    totals = combined_all(stats, "neg", combine_totals)
    coefficient, loss_part = finish_rows(similar, is_positive, totals, neg_place, query_dev)
    query_sum, passage_sum = tile_backward(
        query_tokens, passage_tokens, passage_len, inner_all, coefficient
    )
    query_grad = lax.psum_scatter(query_sum, "neg", scatter_dimension=0, tiled=True)
    emb_sum = lax.psum_scatter(passage_sum, "dp", scatter_dimension=0, tiled=True)
    emb_grad = emb_sum.astype(jnp.bfloat16).reshape(
        passage_dev * emb_sum.shape[1], emb_sum.shape[2]
    )
    residual_grad, context_grad, proj_part, colbert_part, gain_part = window_rows(
        residual, context, emb_grad, out_proj, norm_gain, colbert_proj
    )
    out_proj_grad, colbert_grad, gain_grad, loss_total = lax.psum(
        (proj_part, colbert_part, gain_part, loss_part), ("dp", "neg")
    )
    loss = loss_total / (query_dev * lax.axis_size("dp") * neg_size)
    return (loss, query_grad, residual_grad, context_grad, out_proj_grad, colbert_grad, gain_grad)


def solution(mesh):
    in_specs = (
        P(("dp", "neg"), None, None),
        P(("dp", "neg")),
        P(("dp", "neg"), None, None),
        P(("dp", "neg")),
        P(("dp", "neg"), None),
        P(("dp", "neg"), None),
        P(),
        P(),
        P(),
    )
    out_specs = (
        P(),
        P(("dp", "neg"), None, None),
        P(("dp", "neg"), None),
        P(("dp", "neg"), None),
        P(),
        P(),
        P(),
    )
    return jax.shard_map(body, mesh=mesh, in_specs=in_specs, out_specs=out_specs, check_vma=False)
```

profile of v0, /device:TPU:0, one launch (start us, length us, event | category | flops | bytes accessed | tf_op | source)
XLA Modules:
  0.0 304.9 jit_solution(8071022490365719969)
XLA Ops:
  8.9 1.2 dynamic-slice
  10.1 0.8 dynamic-update-slice
  10.9 9.9 %all-reduce = s32[4]{0:T(128)S(1)} all-reduce(s32[4]{0:T(128)S(1)} %dynamic-update-slice), channel_id=1, replica_groups=mesh['dp'=4,'neg'=8] {'dp'}, use_global_device_ids=true, to_apply=%add | all-reduce | flops 4 | bytes 32
  20.8 16.9 %all_gather.31 = bf16[4,512,128]{2,1,0:T(8,128)(2,1)} all-gather(bf16[1,512,128]{2,1,0:T(8,128)(2,1)} %param.17), channel_id=1, replica_groups=mesh['dp'=4,'neg'=8] {'dp'}, dimensions={0}, use_global_device_ids=true | all-gather | bytes 655360 | tf_op jit(solution)/shard_map/all_gather | solution.py:152
  37.7 9.5 %all_gather.32 = bf16[32,32,128]{2,1,0:T(8,128)(2,1)S(1)} all-gather(bf16[4,32,128]{2,1,0:T(8,128)(2,1)} %param.15), channel_id=1, replica_groups=mesh['dp'=4,'neg'=8] {'neg'}, dimensions={0}, use_global_device_ids=true | all-gather | bytes 294912 | tf_op jit(solution)/shard_map/all_gather | solution.py:148
  47.2 16.2 %while.53 = (s32[]{:T(128)}, f32[4,32,32]{2,1,0:T(8,128)S(1)}, f32[4,32]{1,0:T(4,128)S(1)}, s32[4]{0:T(128)S(1)}, bf16[4,512,128]{2,1,0:T(8,128)(2,1)}, /*index=...) while((s32[]{:T(128)}, f32[4,32,32]{2,1,0:T(8,128)S(1)}, f32[4,32]{1,0:T(4,128)S(1)}, ...), condition=%wide.region_4.5_spmd, body=%wide.region_0.4_spmd.sunk | while | flops 136840672 | bytes 4672013 | solution.py:45
  47.2 0.6 dynamic_slice.119
  47.8 0.6 iota_compare_fusion.4
  48.4 1.4 select_reduce_fusion.2
  49.8 0.4 exponential_reduce_fusion.2
  51.2 0.6 dynamic_slice.119
  51.8 0.6 iota_compare_fusion.4
  52.5 1.4 select_reduce_fusion.2
  53.8 0.4 exponential_reduce_fusion.2
  55.3 0.6 dynamic_slice.119
  55.9 0.6 iota_compare_fusion.4
  56.5 1.4 select_reduce_fusion.2
  57.9 0.4 exponential_reduce_fusion.2
  59.3 0.6 dynamic_slice.119
  59.9 0.6 iota_compare_fusion.4
  60.6 1.4 select_reduce_fusion.2
  61.9 0.4 exponential_reduce_fusion.2
  63.4 0.6 dynamic-slice.1
  64.9 7.1 %all-reduce.3 = s32[32]{0:T(128)S(1)} all-reduce(s32[32]{0:T(128)S(1)} %dynamic-update-slice.3), channel_id=1, replica_groups=mesh['dp'=4,'neg'=8] {'neg'}, use_global_device_ids=true, to_apply=%add.3 | all-reduce | flops 32 | bytes 256
  72.8 0.2 dynamic-update-slice.1
  73.4 11.8 %all-reduce.7 = (f32[256]{0:T(256)S(1)}, f32[256]{0:T(256)S(1)}, f32[256]{0:T(256)S(1)}) all-reduce(f32[256]{0:T(256)S(1)} %dynamic-update-slice.1, f32[256]{0:T(256)S(1)} %dynamic-update-slice.2, f32[256]{0:T(256)S(1)} %dynamic-update-slice.4), channel_id=2, replica_groups=mesh['dp'=4,'neg'=8] {'neg'}, use_global_device_ids=true, to_apply=%add.1 | all-reduce | flops 768 | bytes 6144
  85.5 0.3 while.54
  85.8 25.8 %while.55 = (s32[]{:T(128)}, f32[1024,128]{1,0:T(8,128)}, f32[4,512,128]{2,1,0:T(8,128)}, s32[4]{0:T(128)S(1)}, bf16[4,512,128]{2,1,0:T(8,128)(2,1)}, /*index=5*...) while((s32[]{:T(128)}, f32[1024,128]{1,0:T(8,128)}, ...), condition=%wide.region_13.14_spmd.clone, body=%wide.region_12.13_spmd.clone.sunk | while | flops 405012992 | bytes 5282823 | solution.py:105
  86.1 0.6 dynamic_slice.125
  86.7 0.6 iota_compare_fusion.5
  87.3 1.5 multiply_convert_fusion.5
  88.8 1.2 fusion.63
  90.0 2.2 convolution_add_fusion.2
  92.4 0.6 dynamic_slice.125
  93.0 0.6 iota_compare_fusion.5
  93.6 1.5 multiply_convert_fusion.5
  95.1 1.1 fusion.63
  96.2 2.4 convolution_add_fusion.2
  98.9 0.6 dynamic_slice.125
  99.4 0.6 iota_compare_fusion.5
  100.1 1.5 multiply_convert_fusion.5
  101.6 1.1 fusion.63
  102.7 2.4 convolution_add_fusion.2
  105.3 0.6 dynamic_slice.125
  105.9 0.6 iota_compare_fusion.5
  106.6 1.5 multiply_convert_fusion.5
  108.1 1.1 fusion.63
  109.2 2.4 convolution_add_fusion.2
  111.7 2.9 fusion.36
  114.6 1.3 copy-done.1
  115.9 0.3 multiply_reduce_fusion.2
  116.2 21.0 %reduce-scatter.5.cloned.1.call-done = f32[1,512,128]{2,1,0:T(8,128)} async-done(((f32[4,512,128]{2,1,0:T(8,128)}), f32[1,512,128]{2,1,0:T(8,128)}) %reduce-scatter.5.cloned.1.call-update) | async-done | bytes 262160 | tf_op jit(solution)/shard_map/reduce_scatter | solution.py:168
  137.3 2.7 multiply_reduce_fusion
  140.0 0.6 multiply_convert_fusion.2
  140.6 0.6 copy-done.5
  141.2 3.3 %convolution_bitcast_fusion.1 = f32[1024,1024]{0,1:T(8,128)} fusion(bf16[512,1024]{1,0:T(8,128)(2,1)S(1)} %multiply_convert_fusion.2, bf16[512,1024]{1,0:T(8,128)(2,1)S(1)} %copy-done.5), kind=kOutput, calls=%fused_computation.37 | convolution fusion | flops 1073741824 | bytes 6291456 | tf_op jit(solution)/shard_map/dot_general | solution.py:136
  144.5 1.6 fusion.22
  146.2 0.5 reduce-scatter.3.cloned.1.call-update
  146.7 0.7 dynamic-slice_reduce_fusion
  147.4 39.7 %all-reduce.5 = (f32[]{:T(128)}, f32[1024]{0:T(1024)}) all-reduce(f32[]{:T(128)} %dynamic-slice_reduce_fusion, f32[1024]{0:T(1024)S(1)} %get-tuple-element.355), channel_id=1, replica_groups=mesh['dp'=4,'neg'=8] {'dp','neg'}, use_global_device_ids=true, to_apply=%region_11.12 | all-reduce | flops 1025 | bytes 8200 | tf_op jit(solution)/shard_map/psum | solution.py:175
  187.7 2.3 convolution_convert_fusion
  190.0 100.1 %all-reduce.10.cloned.1.call-done = (f32[1024,1024]{0,1:T(8,128)}, f32[1024,128]{1,0:T(8,128)}) async-done(((f32[1024,1024]{0,1:T(8,128)}, f32[1024,128]{1,0:T(8,128)}), (f32[1024,1024]{0,1:T(8,128)}, f32[1024,128]{1,0:T(8,128)})) %all-reduce.10.cloned.1.call-update) | async-done | bytes 4718608 | tf_op jit(solution)/shard_map/psum | solution.py:175
  290.1 5.4 %copy.18 = f32[1024,1024]{1,0:T(8,128)} copy(f32[1024,1024]{0,1:T(8,128)} %get-tuple-element.404) | data formatting | bytes 8388608
  295.5 0.8 copy.61
  (103 shorter events, 3.6 us)
Async XLA Ops:
  8.0 103.7 %copy-start = (bf16[1024,1024]{1,0:T(8,128)(2,1)S(1)}, bf16[1024,1024]{1,0:T(8,128)(2,1)}, u32[]{:S(2)}) copy-start(bf16[1024,1024]{1,0:T(8,128)(2,1)} %param.21) | copy-start | bytes 6291460
  8.0 129.2 %reduce-scatter.5.cloned.1.call-start = ((), (), s32[]{:S(2)}) async-start(), calls=%async_computation.3 | async-start | bytes 1310720 | tf_op jit(solution)/shard_map/reduce_scatter | solution.py:168
  47.2 16.2 %copy-start.10 = (u32[32]{0:T(128)S(1)}, u32[32]{0:T(128)}, u32[]{:S(2)}) copy-start(u32[32]{0:T(128)} %constant.164) | copy-start | bytes 388
  47.2 17.5 %copy-start.9 = (s32[4]{0:T(128)S(1)}, s32[4]{0:T(128)}, u32[]{:S(2)}) copy-start(s32[4]{0:T(128)} %param.16) | copy-start | bytes 52
  111.6 178.5 %all-reduce.10.cloned.1.call-start = ((), (), s32[]{:S(2)}) async-start(), calls=%async_computation.4 | async-start | bytes 9437184 | tf_op jit(solution)/shard_map/psum | solution.py:175
  114.6 1.3 copy-start.1
  114.6 22.7 %copy-start.7 = (bf16[1024,128]{1,0:T(8,128)(2,1)S(1)}, bf16[1024,128]{1,0:T(8,128)(2,1)}, u32[]{:S(2)}) copy-start(bf16[1024,128]{1,0:T(8,128)(2,1)} %param.23) | copy-start | bytes 786436
  114.6 22.7 %copy-start.8 = (f32[1024]{0:T(1024)S(1)}, f32[1024]{0:T(1024)}, u32[]{:S(2)}) copy-start(f32[1024]{0:T(1024)} %param.22) | copy-start | bytes 12292
  137.3 2.7 copy-start.2
  140.0 1.2 copy-start.5
  141.2 46.5 %copy-start.3 = (bf16[512,1024]{1,0:T(8,128)(2,1)}, bf16[512,1024]{1,0:T(8,128)(2,1)S(1)}, u32[]{:S(2)}) copy-start(bf16[512,1024]{1,0:T(8,128)(2,1)S(1)} %multiply_convert_fusion.2) | copy-start | bytes 3145732
  141.2 3.3 %copy-start.4 = (f32[1,512,128]{2,1,0:T(8,128)S(1)}, f32[1,512,128]{2,1,0:T(8,128)}, u32[]{:S(2)}) copy-start(f32[1,512,128]{2,1,0:T(8,128)} %reduce-scatter.5.cloned.1.call-done) | copy-start | bytes 786436
  146.1 149.4 %reduce-scatter.3.cloned.1.call-start = ((), (), s32[]{:S(2)}) async-start(), calls=%async_computation.2 | async-start | bytes 589824 | tf_op jit(solution)/shard_map/reduce_scatter | solution.py:167
  290.1 5.4 %copy-start.6 = (f32[1024,128]{1,0:T(8,128)S(1)}, f32[1024,128]{1,0:T(8,128)}, u32[]{:S(2)}) copy-start(f32[1024,128]{1,0:T(8,128)} %get-tuple-element.658) | copy-start | bytes 1572868
Sparse Core Ops, SparseCore 0:
  111.7 25.4 reduce-scatter.4
  146.3 143.7 all-reduce.9
Sparse Core Ops, SparseCore 1:
  150.3 32.6 reduce-scatter.2
where the time goes:
time: 306 us; the launch traced here: 305 us
  waiting for transfers between devices  122 us (40%)
  blocking collectives  94.9 us (31%)
  matrix products  38 us (12%)
  between operations  19.5 us (6%)
  local copies, waits for them, and re-layouts  18.2 us (6%)
  other arithmetic  9.43 us (3%)
  loops' own time  3.07 us (1%)
    psum x1, waiting for transfers between devices, body(): lax.psum((proj_part, colbert_part, gain_part, loss_part), ('dp', 'neg'))  100 us
    psum x1, blocking collectives, body(): lax.psum((proj_part, colbert_part, gain_part, loss_part), ('dp', 'neg'))  39.7 us
    unnamed x3, blocking collectives  28.8 us
    reduce_scatter x1, waiting for transfers between devices, body(): lax.psum_scatter(passage_sum, 'dp', scatter_dimension=0, tiled=True)  21 us
    all_gather x1, blocking collectives, body(): lax.all_gather(passage_emb, 'dp', axis=0, tiled=True)  16.9 us
    unnamed x36, local copies, waits for them, and re-layouts  11.6 us
    dot_general x8, matrix products, masked_scores(): jnp.einsum('rd,jd->rj', query_block, passage_one, preferred_element_type=...  11.4 us
    all_gather x1, blocking collectives, body(): lax.all_gather(query_emb, 'neg', axis=0, tiled=True)  9.51 us
  transfers between devices with their start and end apart: 3, of which 2 were waited for; matrix products, arithmetic and copies ran while one was open for 4% of the time, Pallas kernels for 0%

commit v1 on v0

--- a/solution.py
+++ b/solution.py
@@ -173,7 +173,7 @@
         residual, context, emb_grad, out_proj, norm_gain, colbert_proj
     )
     out_proj_grad, colbert_grad, gain_grad, loss_total = lax.psum(
-        (proj_part, colbert_part, gain_part, loss_part), ("dp", "neg")
+        lax.psum((proj_part, colbert_part, gain_part, loss_part), "neg"), "dp"
     )
     loss = loss_total / (query_dev * lax.axis_size("dp") * neg_size)
     return (loss, query_grad, residual_grad, context_grad, out_proj_grad, colbert_grad, gain_grad)

time: 306 us -> 451 us (1.47)
  waiting for transfers between devices: 122 us -> 281 us
  blocking collectives: 94.9 us -> 82.6 us
    psum x1 -> x2, waiting for transfers between devices: 100 us -> 229 us  [the longest x1 143 us: body(): lax.psum(lax.psum((proj_part, colbert_part, gain_part, loss_part), 'neg')...]
    reduce_scatter x1, waiting for transfers between devices: 0.01 us -> 31.2 us  [body(): lax.psum_scatter(query_sum, 'neg', scatter_dimension=0, tiled=True)]
    psum x1 -> x2, blocking collectives: 39.7 us -> 27.4 us  [the longest x1 13.7 us: body(): lax.psum((proj_part, colbert_part, gain_part, loss_part), 'neg')]
  transfers between devices with their start and end apart: 3 -> 4, of which waited for: 2 -> 4; matrix products, arithmetic and copies ran while one was open for 4% -> 3% of each run, Pallas kernels for 0% -> 0%
where the time goes in v1:
time: 451 us
  waiting for transfers between devices  281 us (62%)
  blocking collectives  82.6 us (18%)
  matrix products  38 us (8%)
  local copies, waits for them, and re-layouts  18.2 us (4%)
  between operations  17.8 us (4%)
  other arithmetic  9.43 us (2%)
    psum x1, waiting for transfers between devices, body(): lax.psum(lax.psum((proj_part, colbert_part, gain_part, loss_part), 'neg')...  143 us
    psum x1, waiting for transfers between devices, body(): lax.psum((proj_part, colbert_part, gain_part, loss_part), 'neg')  85.2 us
    reduce_scatter x1, waiting for transfers between devices, body(): lax.psum_scatter(query_sum, 'neg', scatter_dimension=0, tiled=True)  31.2 us
    unnamed x3, blocking collectives  28.8 us
    reduce_scatter x1, waiting for transfers between devices, body(): lax.psum_scatter(passage_sum, 'dp', scatter_dimension=0, tiled=True)  21 us
    all_gather x1, blocking collectives, body(): lax.all_gather(passage_emb, 'dp', axis=0, tiled=True)  16.9 us
    psum x1, blocking collectives, body(): lax.psum((proj_part, colbert_part, gain_part, loss_part), 'neg')  13.7 us
    psum x1, blocking collectives, body(): lax.psum(lax.psum((proj_part, colbert_part, gain_part, loss_part), 'neg')...  13.7 us
  transfers between devices with their start and end apart: 4, of which 4 were waited for; matrix products, arithmetic and copies ran while one was open for 3% of the time, Pallas kernels for 0%

profile of v1, /device:TPU:0, one launch (start us, length us, event | category | flops | bytes accessed | tf_op | source)
XLA Modules:
  0.0 450.6 jit_solution(3994956664222402439)
XLA Ops:
  8.0 1.2 dynamic-slice
  9.3 0.8 dynamic-update-slice
  10.0 9.9 %all-reduce = s32[4]{0:T(128)S(1)} all-reduce(s32[4]{0:T(128)S(1)} %dynamic-update-slice), channel_id=1, replica_groups=mesh['dp'=4,'neg'=8] {'dp'}, use_global_device_ids=true, to_apply=%add | all-reduce | flops 4 | bytes 32
  20.0 16.9 %all_gather.31 = bf16[4,512,128]{2,1,0:T(8,128)(2,1)} all-gather(bf16[1,512,128]{2,1,0:T(8,128)(2,1)} %param.17), channel_id=1, replica_groups=mesh['dp'=4,'neg'=8] {'dp'}, dimensions={0}, use_global_device_ids=true | all-gather | bytes 655360 | tf_op jit(solution)/shard_map/all_gather | solution.py:152
  36.8 9.5 %all_gather.32 = bf16[32,32,128]{2,1,0:T(8,128)(2,1)S(1)} all-gather(bf16[4,32,128]{2,1,0:T(8,128)(2,1)} %param.15), channel_id=1, replica_groups=mesh['dp'=4,'neg'=8] {'neg'}, dimensions={0}, use_global_device_ids=true | all-gather | bytes 294912 | tf_op jit(solution)/shard_map/all_gather | solution.py:148
  46.3 16.2 %while.53 = (s32[]{:T(128)}, f32[4,32,32]{2,1,0:T(8,128)S(1)}, f32[4,32]{1,0:T(4,128)S(1)}, s32[4]{0:T(128)S(1)}, bf16[4,512,128]{2,1,0:T(8,128)(2,1)}, /*index=...) while((s32[]{:T(128)}, f32[4,32,32]{2,1,0:T(8,128)S(1)}, f32[4,32]{1,0:T(4,128)S(1)}, ...), condition=%wide.region_4.5_spmd, body=%wide.region_0.4_spmd.sunk | while | flops 136840672 | bytes 4672013 | solution.py:45
  46.3 0.6 dynamic_slice.119
  46.9 0.6 iota_compare_fusion.4
  47.6 1.4 select_reduce_fusion.2
  48.9 0.4 exponential_reduce_fusion.2
  50.4 0.6 dynamic_slice.119
  51.0 0.6 iota_compare_fusion.4
  51.6 1.4 select_reduce_fusion.2
  53.0 0.4 exponential_reduce_fusion.2
  54.5 0.6 dynamic_slice.119
  55.0 0.6 iota_compare_fusion.4
  55.7 1.4 select_reduce_fusion.2
  57.0 0.4 exponential_reduce_fusion.2
  58.5 0.6 dynamic_slice.119
  59.1 0.6 iota_compare_fusion.4
  59.7 1.4 select_reduce_fusion.2
  61.1 0.4 exponential_reduce_fusion.2
  62.6 0.6 dynamic-slice.1
  64.1 7.1 %all-reduce.3 = s32[32]{0:T(128)S(1)} all-reduce(s32[32]{0:T(128)S(1)} %dynamic-update-slice.3), channel_id=1, replica_groups=mesh['dp'=4,'neg'=8] {'neg'}, use_global_device_ids=true, to_apply=%add.3 | all-reduce | flops 32 | bytes 256
  72.6 11.8 %all-reduce.6 = (f32[256]{0:T(256)S(1)}, f32[256]{0:T(256)S(1)}, f32[256]{0:T(256)S(1)}) all-reduce(f32[256]{0:T(256)S(1)} %dynamic-update-slice.1, f32[256]{0:T(256)S(1)} %dynamic-update-slice.2, f32[256]{0:T(256)S(1)} %dynamic-update-slice.4), channel_id=2, replica_groups=mesh['dp'=4,'neg'=8] {'neg'}, use_global_device_ids=true, to_apply=%add.1 | all-reduce | flops 768 | bytes 6144
  85.0 25.8 %while.55 = (s32[]{:T(128)}, f32[1024,128]{1,0:T(8,128)}, f32[4,512,128]{2,1,0:T(8,128)}, s32[4]{0:T(128)S(1)}, bf16[4,512,128]{2,1,0:T(8,128)(2,1)}, /*index=5*...) while((s32[]{:T(128)}, f32[1024,128]{1,0:T(8,128)}, ...), condition=%wide.region_14.15_spmd.clone, body=%wide.region_13.14_spmd.clone.sunk | while | flops 405012992 | bytes 5282823 | solution.py:105
  85.2 0.6 dynamic_slice.125
  85.8 0.6 iota_compare_fusion.5
  86.5 1.5 multiply_convert_fusion.5
  88.0 1.2 fusion.63
  89.1 2.2 convolution_add_fusion.2
  91.5 0.6 dynamic_slice.125
  92.1 0.6 iota_compare_fusion.5
  92.8 1.5 multiply_convert_fusion.5
  94.3 1.1 fusion.63
  95.4 2.4 convolution_add_fusion.2
  98.0 0.6 dynamic_slice.125
  98.6 0.6 iota_compare_fusion.5
  99.3 1.5 multiply_convert_fusion.5
  100.7 1.1 fusion.63
  101.9 2.4 convolution_add_fusion.2
  104.5 0.6 dynamic_slice.125
  105.1 0.6 iota_compare_fusion.5
  105.7 1.5 multiply_convert_fusion.5
  107.2 1.1 fusion.63
  108.4 2.4 convolution_add_fusion.2
  110.8 2.9 fusion.36
  113.8 1.3 copy-done.1
  115.4 21.0 %reduce-scatter.5.cloned.1.call-done = f32[1,512,128]{2,1,0:T(8,128)} async-done(((f32[4,512,128]{2,1,0:T(8,128)}), f32[1,512,128]{2,1,0:T(8,128)}) %reduce-scatter.5.cloned.1.call-update) | async-done | bytes 262160 | tf_op jit(solution)/shard_map/reduce_scatter | solution.py:168
  136.4 2.7 multiply_reduce_fusion
  139.2 0.6 multiply_convert_fusion.2
  139.8 0.6 copy-done.5
  140.4 3.3 convolution_bitcast_fusion.1
  143.7 1.6 fusion.22
  145.4 85.2 %all-reduce.13.cloned.1.call-done = (f32[1024,1024]{0,1:T(8,128)}, f32[1024,128]{1,0:T(8,128)}) async-done(((f32[1024,1024]{0,1:T(8,128)}, f32[1024,128]{1,0:T(8,128)}), (f32[1024,1024]{0,1:T(8,128)}, f32[1024,128]{1,0:T(8,128)})) %all-reduce.13.cloned.1.call-update) | async-done | bytes 4718608 | tf_op jit(solution)/shard_map/psum | solution.py:176
  230.6 0.5 reduce-scatter.3.cloned.1.call-update
  231.2 0.7 dynamic-slice_reduce_fusion
  231.8 13.7 %all-reduce.5 = (f32[]{:T(128)}, f32[1024]{0:T(1024)S(1)}) all-reduce(f32[]{:T(128)} %dynamic-slice_reduce_fusion, f32[1024]{0:T(1024)S(1)} %get-tuple-element.355), channel_id=1, replica_groups=mesh['dp'=4,'neg'=8] {'neg'}, use_global_device_ids=true, to_apply=%region_11.12 | all-reduce | flops 1025 | bytes 8200 | tf_op jit(solution)/shard_map/psum | solution.py:176
  245.6 13.7 %all-reduce.8 = (f32[]{:T(128)}, f32[1024]{0:T(1024)}) all-reduce(f32[]{:T(128)} %get-tuple-element.402, f32[1024]{0:T(1024)S(1)} %get-tuple-element.403), channel_id=1, replica_groups=mesh['dp'=4,'neg'=8] {'dp'}, use_global_device_ids=true, to_apply=%region_12.13 | all-reduce | flops 1025 | bytes 8200 | tf_op jit(solution)/shard_map/psum | solution.py:175
  259.9 2.3 convolution_convert_fusion
  262.1 143.4 %all-reduce.15.cloned.1.call-done = (f32[1024,1024]{0,1:T(8,128)}, f32[1024,128]{1,0:T(8,128)}) async-done(((f32[1024,1024]{0,1:T(8,128)}, f32[1024,128]{1,0:T(8,128)}), (f32[1024,1024]{0,1:T(8,128)}, f32[1024,128]{1,0:T(8,128)})) %all-reduce.15.cloned.1.call-update) | async-done | bytes 4718608 | tf_op jit(solution)/shard_map/psum | solution.py:175
  405.5 5.4 %copy.18 = f32[1024,1024]{1,0:T(8,128)} copy(f32[1024,1024]{0,1:T(8,128)} %get-tuple-element.411) | data formatting | bytes 8388608
  410.9 31.2 %reduce-scatter.3.cloned.1.call-done = f32[4,32,128]{2,1,0:T(8,128)} async-done(((f32[32,32,128]{2,1,0:T(8,128)}), f32[4,32,128]{2,1,0:T(8,128)}) %reduce-scatter.3.cloned.1.call-update) | async-done | bytes 65552 | tf_op jit(solution)/shard_map/reduce_scatter | solution.py:167
  442.1 0.8 copy.63
  (107 shorter events, 4.6 us)
Async XLA Ops:
  7.2 103.7 %copy-start = (bf16[1024,1024]{1,0:T(8,128)(2,1)S(1)}, bf16[1024,1024]{1,0:T(8,128)(2,1)}, u32[]{:S(2)}) copy-start(bf16[1024,1024]{1,0:T(8,128)(2,1)} %param.21) | copy-start | bytes 6291460
  7.2 129.3 %reduce-scatter.5.cloned.1.call-start = ((), (), s32[]{:S(2)}) async-start(), calls=%async_computation.3 | async-start | bytes 1310720 | tf_op jit(solution)/shard_map/reduce_scatter | solution.py:168
  46.3 16.2 %copy-start.10 = (u32[32]{0:T(128)S(1)}, u32[32]{0:T(128)}, u32[]{:S(2)}) copy-start(u32[32]{0:T(128)} %constant.164) | copy-start | bytes 388
  46.3 17.5 %copy-start.9 = (s32[4]{0:T(128)S(1)}, s32[4]{0:T(128)}, u32[]{:S(2)}) copy-start(s32[4]{0:T(128)} %param.16) | copy-start | bytes 52
  110.8 119.8 %all-reduce.13.cloned.1.call-start = ((), (), s32[]{:S(2)}) async-start(), calls=%async_computation.4 | async-start | bytes 9437184 | tf_op jit(solution)/shard_map/psum | solution.py:176
  113.7 1.3 copy-start.1
  113.7 22.7 %copy-start.7 = (bf16[1024,128]{1,0:T(8,128)(2,1)S(1)}, bf16[1024,128]{1,0:T(8,128)(2,1)}, u32[]{:S(2)}) copy-start(bf16[1024,128]{1,0:T(8,128)(2,1)} %param.23) | copy-start | bytes 786436
  113.7 22.7 %copy-start.8 = (f32[1024]{0:T(1024)S(1)}, f32[1024]{0:T(1024)}, u32[]{:S(2)}) copy-start(f32[1024]{0:T(1024)} %param.22) | copy-start | bytes 12292
  136.4 2.7 copy-start.2
  139.2 1.2 copy-start.5
  140.4 119.5 %copy-start.3 = (bf16[512,1024]{1,0:T(8,128)(2,1)}, bf16[512,1024]{1,0:T(8,128)(2,1)S(1)}, u32[]{:S(2)}) copy-start(bf16[512,1024]{1,0:T(8,128)(2,1)S(1)} %multiply_convert_fusion.2) | copy-start | bytes 3145732
  140.4 3.3 copy-start.4
  145.3 260.2 %all-reduce.15.cloned.1.call-start = ((), (), s32[]{:S(2)}) async-start(), calls=%async_computation.5 | async-start | bytes 9437184 | tf_op jit(solution)/shard_map/psum | solution.py:175
  230.6 211.5 %reduce-scatter.3.cloned.1.call-start = ((), (), s32[]{:S(2)}) async-start(), calls=%async_computation.2 | async-start | bytes 589824 | tf_op jit(solution)/shard_map/reduce_scatter | solution.py:167
  405.5 36.6 %copy-start.6 = (f32[1024,128]{1,0:T(8,128)S(1)}, f32[1024,128]{1,0:T(8,128)}, u32[]{:S(2)}) copy-start(f32[1024,128]{1,0:T(8,128)} %get-tuple-element.662) | copy-start | bytes 1572868
Sparse Core Ops, SparseCore 0:
  110.9 25.4 reduce-scatter.4
  145.4 85.0 all-reduce.12
  233.0 172.4 all-reduce.14
  409.0 33.0 reduce-scatter.2
